TPU v7x, 32 devices: a whole 2x2x4 slice. The times are simulated.
32 devices in a mesh: blk: 8 (over z, y), col: 4 (over x, core).
Axes of the slice: x: 2, y: 2, z: 4, core: 2. Of those that a mesh axis runs over, the one named last changes fastest.
Arguments:
- spectra: bfloat16 [64, 128, 256], P(('blk', 'col')), may hold values from -5 to 5
- kernels: bfloat16 [60, 128, 256], replicated, may hold values from -5 to 5
- weights: float32 [60], replicated, may hold values from 0.3 to 1
- hotspot_flags: int32 [64], P(('blk', 'col')), may hold values from 0 to 1, as said below
- helper_map: int32 [64], P(('blk', 'col')), may hold values from 0 to 3, as said below
- kernel_counts: int32 [64], P(('blk', 'col')), may hold values from 6 to 12
Outputs:
- aerial_images: float32 [64, 256, 256], P(('blk', 'col'))
- pending: float32 [8, 4], P('blk', 'col')
Inputs may be any that keep to these rules, and one draw needn't show every extreme that they name: `hotspot_flags`: some device has all its 2 tiles flagged in every draw. `helper_map`: among one device's flagged tiles at most 1 name the same value, and in every draw some device has exactly 1 flagged tiles naming one value.
All inputs are finite; a program needn't handle non-finite values.
Results may differ from a plain program's by a relative error of at most 0.0037.
Values may be sent and summed in bfloat16 or wider, within the bound.
No kernel may reach another device: no remote copies, remote signals or barrier semaphores. Data moves between devices by JAX's collectives and lax.ppermute only.
A program may use at most 64 MiB of HBM per device.

v0:
```python
import math

import jax
import jax.numpy as jnp
import numpy as np
from jax import lax
from jax.experimental import pallas as pl
from jax.experimental.pallas import tpu as pltpu
from jax.sharding import PartitionSpec as P

Q = 256
KB = 6


def make_table(band_width, length):
    row_index = np.arange(length, dtype=np.int32)[:, None]
    col_index = np.arange(band_width, dtype=np.int32)[None, :] - band_width // 2
    angle = np.mod(row_index * col_index, length).astype(np.float64) * (2.0 * math.pi / length)
    scale = 1.0 / math.sqrt(band_width)
    real = (np.cos(angle) * scale).astype(np.float32).T
    imag = (np.sin(angle) * scale).astype(np.float32).T
    table = np.block([[real, imag], [-imag, real]])
    return jnp.asarray(table).astype(jnp.bfloat16)


def plan(core, flags, counts, kern_total):
    numbers, firsts, starts = [], [], [jnp.int32(0)]
    most = jnp.int32(0)
    for f, c in zip(flags, counts):
        for t in range(f.shape[0]):
            n = jnp.where(f[t] == 1, kern_total, c[t])
            first = lax.rem(core + t, 2)
            blocks = (n + KB - 1) // KB
            most = jnp.maximum(most, blocks)
            numbers.append(n)
            firsts.append(first)
            starts.append(starts[-1] + (blocks - first + 1) // 2)
    return numbers, firsts, starts, most


def run_blocks(low, high, lists, kbuf, tbuf, both, ws, img, half, accs, prepare, ready, ahead):
    numbers, firsts, starts, _ = lists
    width, length = kbuf.shape[1], img.shape[1]
    a0, a1, b0, b1 = accs[0:2], accs[2:4], accs[4:7], accs[7:10]

    def place(i):
        j, start, first, n = jnp.int32(0), starts[0], firsts[0], numbers[0]
        for q in range(1, len(numbers)):
            take = i >= starts[q]
            j = jnp.where(take, q, j)
            start = jnp.where(take, starts[q], start)
            first = jnp.where(take, firsts[q], first)
            n = jnp.where(take, numbers[q], n)
        return j, first + 2 * (i - start), n

    def stage_one(j, k, slot, first=False):
        kb = kbuf[k].astype(jnp.float32)
        kr, ki = kb[:, :width], kb[:, width:]
        sp = both[j].astype(jnp.float32)
        sr, si = sp[:, :width], sp[:, width:]
        band = jnp.concatenate([kr * sr - ki * si, kr * si + ki * sr], 1).astype(jnp.bfloat16)
        load = 0 if first else None
        pltpu.matmul_acc_lhs(a0[slot], band, load_staged_rhs=load)
        pltpu.matmul_acc_lhs(a1[slot], band, load_staged_rhs=load)

    def middle(slot):
        hr = pltpu.matmul_pop(a0[slot]).astype(jnp.bfloat16)
        hi = pltpu.matmul_pop(a1[slot]).astype(jnp.bfloat16)
        return jnp.concatenate([hr.T, hi.T], 1)

    def stage_two(data, slot):
        pltpu.matmul_acc_lhs(b0[slot], data)
        pltpu.matmul_acc_lhs(b1[slot], data)

    def finish(j, k, n, slot):
        w = jnp.where(k < n, ws[0, k], 0.0)
        fr = pltpu.matmul_pop(b0[slot])
        fi = pltpu.matmul_pop(b1[slot])
        img[j] = img[j] + w * (fr * fr + fi * fi)

    prepare()
    pltpu.matmul_push_rhs(tbuf[:, :length], staging_register=0, mxu_index=0)
    pltpu.matmul_push_rhs(tbuf[:, length:], staging_register=0, mxu_index=1)
    j, b, _ = place(low)
    stage_one(j, b * KB, 0, first=True)
    stage_one(j, b * KB + 1, 1)
    half[...] = middle(0)

    def block(i, here):
        j, b, n = place(i)
        jn, bn, _ = place(jnp.minimum(i + 1, high - 1))
        jp, bp, np_ = place(jnp.maximum(i - 1, low))
        if ready is not None:

            @pl.when(bn >= here)
            def _():
                lax.fori_loop(here, bn + 1, ready, 0)

        data = half[...]
        for u in range(KB):
            if u + 2 < KB:
                stage_one(j, b * KB + u + 2, u % 2)
            else:
                stage_one(jn, bn * KB + (u + 2 - KB), u % 2)
            stage_two(data, u % 3)
            data = middle((u + 1) % 2)
            if u < 2:
                finish(jp, bp * KB + KB - 2 + u, np_, (u + 1) % 3)
            else:
                finish(j, b * KB + u - 2, n, (u + 1) % 3)
        half[...] = data
        return jnp.maximum(here, bn + 1)

    here = lax.fori_loop(low, high, block, jnp.int32(ahead))
    j, b, n = place(jnp.maximum(high - 1, low))
    finish(j, b * KB + KB - 2, n, 1)
    finish(j, b * KB + KB - 1, n, 2)
    pltpu.matmul_pop(a0[1])
    pltpu.matmul_pop(a1[1])
    return here


def with_accs(body, width, length):
    pl.run_scoped(
        body,
        *[pltpu.ACC(0)((width, length), jnp.float32)] * 2,
        *[pltpu.ACC(1)((width, length), jnp.float32)] * 2,
        *[pltpu.ACC(0)((length, length), jnp.float32)] * 3,
        *[pltpu.ACC(1)((length, length), jnp.float32)] * 3,
    )


def first_kernel(pflags, pcounts, phelper, pspectra, flags, counts, helper, weights, spectra, kernels, table,
                 img, kbuf, tbuf, both, across, above, below, base, fl, cn, hm, ws, half, ksem, sems):
    tiles, width, _ = spectra.shape
    length = img.shape[1]
    kern_total = kernels.shape[0]
    core = lax.rem(lax.axis_index("col"), 2)
    pairs = [(flags, fl), (counts, cn), (helper, hm), (weights, ws), (table, tbuf), (spectra, both.at[pl.ds(0, tiles)])]
    copies = [pltpu.make_async_copy(src, dst, sems.at[i]) for i, (src, dst) in enumerate(pairs)]

    def chunk(b):
        part = pl.ds(b * KB, KB)
        return pltpu.make_async_copy(kernels.at[part], kbuf.at[part], ksem.at[b])

    def start_chunk(b, c):
        chunk(b).start()
        return c

    def wait_chunk(b, c):
        chunk(b).wait()
        return c

    for copy in copies:
        copy.start()
    for b in range(2):
        chunk(b).start()
    img[...] = jnp.zeros_like(img)
    both[tiles:] = pspectra[...]

    def body(*accs):
        for acc in accs:
            pltpu.matmul_pop(acc)
        for copy in copies[:3]:
            copy.wait()
        lists = plan(core, (fl, pflags), (cn, pcounts), kern_total)
        _, _, starts, most = lists
        lax.fori_loop(2, most, start_chunk, 0)
        odd_row = lax.rem(lax.axis_index("blk"), 2)

        def handed(f, h, direction):
            value = jnp.float32(0)
            for t in range(tiles):
                value = value + jnp.where((f[t] == 1) & (h[t] == direction), jnp.float32(kern_total), 0.0)
            return value

        across[...] = jnp.full(across.shape, handed(fl, hm, 3 - core))
        above[...] = jnp.full(above.shape, handed(fl, hm, odd_row))
        below[...] = jnp.full(below.shape, handed(fl, hm, 1 - odd_row))
        kept = handed(pflags, phelper, 3 - core)
        for t in range(tiles):
            kept = kept + jnp.where(fl[t] == 1, 0, cn[t]).astype(jnp.float32)
        base[...] = jnp.full(base.shape, kept)

        def prepare():
            for copy in copies[3:]:
                copy.wait()
            for b in range(2):
                chunk(b).wait()

        split = (2 * starts[-1] + 2) // 3
        here = run_blocks(jnp.int32(0), split, lists, kbuf, tbuf, both, ws, img, half, accs, prepare, wait_chunk, 2)
        lax.fori_loop(here, most, wait_chunk, 0)

    with_accs(body, width, length)


def second_kernel(pflags, pcounts, flags, counts, weights, kbuf, tbuf, both, img_in, own_out, peer_out,
                  fl, cn, ws, wv, half, img, sems):
    tiles = own_out.shape[0]
    kern_total, width, _ = kbuf.shape
    length = img.shape[1]
    core = lax.rem(lax.axis_index("col"), 2)
    pairs = [(flags, fl), (counts, cn), (weights, ws), (weights, wv)]
    copies = [pltpu.make_async_copy(src, dst, sems.at[i]) for i, (src, dst) in enumerate(pairs)]
    for copy in copies:
        copy.start()
    img[...] = img_in[...]

    def body(*accs):
        for acc in accs:
            pltpu.matmul_pop(acc)
        for copy in copies:
            copy.wait()
        lists = plan(core, (fl, pflags), (cn, pcounts), kern_total)
        numbers, _, starts, _ = lists
        split = (2 * starts[-1] + 2) // 3
        run_blocks(split, starts[-1], lists, kbuf, tbuf, both, ws, img, half, accs, lambda: None, None, 0)
        lane = lax.broadcasted_iota(jnp.int32, (1, kern_total), 1)
        for j in range(2 * tiles):
            weight = jnp.sum(jnp.where(lane < numbers[j], wv[...], 0.0), axis=1, keepdims=True)
            dest = own_out if j < tiles else peer_out
            dest[j % tiles] = img[j].T * (1.0 / weight)

    with_accs(body, width, length)


def on_device(spectra, kernels, weights, hotspot_flags, helper_map, kernel_counts):
    tiles, width, _ = spectra.shape
    kern_total = kernels.shape[0]
    rows, cols = lax.axis_size("blk"), lax.axis_size("col")
    table = make_table(width, Q)

    def pairs(size, first):
        return [p for i in range(first, size, 2) for p in ((i, (i + 1) % size), ((i + 1) % size, i))]

    twin = pairs(cols, 0)
    pspectra = lax.ppermute(spectra, "col", twin)
    pflags = lax.ppermute(hotspot_flags, "col", twin)
    pcounts = lax.ppermute(kernel_counts, "col", twin)
    phelper = lax.ppermute(helper_map, "col", twin)

    smem = pl.BlockSpec(memory_space=pltpu.SMEM)
    vmem = pl.BlockSpec(memory_space=pltpu.VMEM)
    hbm = pl.BlockSpec(memory_space=pltpu.HBM)

    def far(*arrays):
        return [pltpu.with_memory_space_constraint(x, pltpu.HBM) for x in arrays]

    f32, bf16 = jnp.float32, jnp.bfloat16
    image = jax.ShapeDtypeStruct((tiles, Q, Q), f32)
    images = jax.ShapeDtypeStruct((2 * tiles, Q, Q), f32)
    wide = jax.ShapeDtypeStruct((8, 128), f32)
    wrow = weights.reshape(1, -1)
    ints = pltpu.SMEM((tiles,), jnp.int32)
    row_smem = pltpu.SMEM((1, kern_total), f32)
    params = pltpu.CompilerParams(vmem_limit_bytes=16 * 2**20)
    half = pltpu.VMEM((Q, 2 * width), bf16)
    cost = pl.CostEstimate(flops=10**10, transcendentals=0, bytes_accessed=10**6)
    img, kbuf, tbuf, both, across, above, below, base = pl.pallas_call(
        first_kernel,
        out_shape=[
            images,
            jax.ShapeDtypeStruct(kernels.shape, bf16),
            jax.ShapeDtypeStruct(table.shape, bf16),
            jax.ShapeDtypeStruct((2 * tiles, width, 2 * width), bf16),
        ]
        + [wide] * 4,
        in_specs=[smem] * 3 + [vmem] + [hbm] * 7,
        out_specs=[vmem] * 8,
        scratch_shapes=[
            ints,
            ints,
            ints,
            row_smem,
            half,
            pltpu.SemaphoreType.DMA((kern_total // KB,)),
            pltpu.SemaphoreType.DMA((6,)),
        ],
        compiler_params=params,
        cost_estimate=cost,
        name="first",
    )(pflags, pcounts, phelper, pspectra, *far(hotspot_flags, kernel_counts, helper_map, wrow, spectra, kernels, table))
    got = [lax.ppermute(below, "blk", pairs(rows, 1))]
    got.append(lax.ppermute(above, "blk", pairs(rows, 0)))
    got.append(lax.ppermute(across, "col", pairs(cols, 1)))
    rest = pl.pallas_call(
        second_kernel,
        out_shape=[image, image],
        in_specs=[smem] * 2 + [hbm] * 3 + [vmem] * 4,
        out_specs=[vmem] * 2,
        scratch_shapes=[
            ints,
            ints,
            row_smem,
            pltpu.VMEM((1, kern_total), f32),
            half,
            pltpu.VMEM((2 * tiles, Q, Q), f32),
            pltpu.SemaphoreType.DMA((4,)),
        ],
        compiler_params=params,
        cost_estimate=cost,
        name="second",
    )
    own, peer = rest(pflags, pcounts, *far(hotspot_flags, kernel_counts, wrow), kbuf, tbuf, both, img)
    other = lax.ppermute(peer, "col", twin)
    pending = jnp.max((base + got[0] + got[1] + got[2]) / kern_total, keepdims=True)
    return own + other, pending


def solution(mesh):
    in_specs = (
        P(("blk", "col"), None, None),
        P(),
        P(),
        P(("blk", "col")),
        P(("blk", "col")),
        P(("blk", "col")),
    )
    out_specs = (P(("blk", "col"), None, None), P("blk", "col"))
    return jax.shard_map(on_device, mesh=mesh, in_specs=in_specs, out_specs=out_specs, check_vma=False)
```

profile of v0, /device:TPU:19, one launch (start us, length us, event | category | flops | bytes accessed | tf_op | source)
XLA Modules:
  0.0 27.0 jit_solution(3902839492393568041)
XLA Ops:
  0.6 0.7 %collective-permute-start.3 = (bf16[2,128,256]{2,1,0:T(8,128)(2,1)}, bf16[2,128,256]{2,1,0:T(8,128)(2,1)S(1)}, u32[]{:S(2)}, u32[]{:S(2)}) collective-permute-start(bf16[2,128,256]{2,1,0:T(8,128)(2,1)} %spectra.1), channel_id=1, source_target_pairs={{0,1},{1,0},{2,3},{3,2},{4,5},{5,4},{6,7},{7,6},{8,9},{9,8},{10,11... | collective-permute-start | bytes 393224 | tf_op jit(solution)/shard_map/ppermute | solution.py:238
  1.4 0.1 collective-permute-start
  1.4 0.4 %collective-permute-start.1 = (s32[2]{0:T(128)}, s32[2]{0:T(128)S(1)}, u32[]{:S(2)}, u32[]{:S(2)}) collective-permute-start(s32[2]{0:T(128)} %counts.3), channel_id=1, source_target_pairs={{0,1},{1,0},{2,3},{3,2},{4,5},{5,4},{6,7},{7,6},{8,9},{9,8},{10,11... | collective-permute-start | bytes 32 | tf_op jit(solution)/shard_map/ppermute | solution.py:240
  1.9 0.1 collective-permute-start.2
  2.0 0.7 %collective-permute-done.pflags = s32[2]{0:T(128)S(1)} collective-permute-done((s32[2]{0:T(128)}, s32[2]{0:T(128)S(1)}, u32[]{:S(2)}, u32[]{:S(2)}) %collective-permute-start) | collective-permute-done | bytes 40 | tf_op jit(solution)/shard_map/ppermute | solution.py:239
  2.7 0.2 collective-permute-done.1.pcounts
  2.8 0.3 %collective-permute-done.2.phelper = s32[2]{0:T(128)S(1)} collective-permute-done((s32[2]{0:T(128)}, s32[2]{0:T(128)S(1)}, u32[]{:S(2)}, u32[]{:S(2)}) %collective-permute-start.2) | collective-permute-done | bytes 40 | tf_op jit(solution)/shard_map/ppermute | solution.py:241
  3.2 0.0 collective-permute-done.3.pspectra
  3.2 4.5 %first.1 = (f32[4,256,256]{2,1,0:T(8,128)S(1)}, bf16[60,128,256]{2,1,0:T(8,128)(2,1)S(1)}, bf16[256,512]{1,0:T(8,128)(2,1)S(1)}, bf16[4,128,256]{2,1,0:T(8,128)(...) custom-call(s32[2]{0:T(128)S(1)} %collective-permute-done.pflags, ...), custom_call_target="tpu_custom_call" | custom-call | flops 10000000000 | bytes 1000000 | tf_op jit(solution)/shard_map/first/pallas_call | solution.py:260
  7.7 2.8 %second.1 = (f32[2,256,256]{2,1,0:T(8,128)S(1)}, f32[2,256,256]{2,1,0:T(8,128)S(1)}) custom-call(s32[2]{0:T(128)S(1)} %collective-permute-done.pflags, s32[2]{0:T(128)S(1)} %collective-permute-done.1.pcounts, s32[2]{0:T(128)} %flags.3, s32[2]{0:T(128)} %counts.3, f32[1,60]{1,0:T(1,128)} %bitcast.3, bf16[60,128,256]{2,1,0:T(8,128)(2,1)S(1)} %get-tuple-element.12.kbuf, ...), custom_call_target="tpu_custom_call" | custom-call | flops 10000000000 | bytes 1000000 | tf_op jit(solution)/shard_map/second/pallas_call | solution.py:305
  10.6 0.2 collective-permute-start.4
  10.8 1.0 %collective-permute-start.5 = (f32[8,128]{1,0:T(8,128)S(1)}, f32[8,128]{1,0:T(8,128)S(1)}, u32[]{:S(2)}, u32[]{:S(2)}) collective-permute-start(f32[8,128]{1,0:T(8,128)S(1)} %get-tuple-element.19), channel_id=1, source_target_pairs={{4,8},{8,4},{12,16},{16,12},{20,24},{24,20},{28,0},{0,28},{5,9},{9... | collective-permute-start | bytes 12296 | tf_op jit(solution)/shard_map/ppermute | solution.py:284
  11.8 10.4 %collective-permute-start.6 = (f32[8,128]{1,0:T(8,128)S(1)}, f32[8,128]{1,0:T(8,128)S(1)}, u32[]{:S(2)}, u32[]{:S(2)}) collective-permute-start(f32[8,128]{1,0:T(8,128)S(1)} %get-tuple-element.20), channel_id=1, source_target_pairs={{0,4},{4,0},{8,12},{12,8},{16,20},{20,16},{24,28},{28,24},{1,5},{5... | collective-permute-start | bytes 12296 | tf_op jit(solution)/shard_map/ppermute | solution.py:285
  22.2 0.0 collective-permute-start.7
  22.2 0.0 collective-permute-done.5
  22.2 1.0 %collective-permute-done.6 = f32[8,128]{1,0:T(8,128)S(1)} collective-permute-done((f32[8,128]{1,0:T(8,128)S(1)}, f32[8,128]{1,0:T(8,128)S(1)}, u32[]{:S(2)}, u32[]{:S(2)}) %collective-permute-start.6) | collective-permute-done | bytes 4128 | tf_op jit(solution)/shard_map/ppermute | solution.py:285
  23.2 2.3 %collective-permute-done.7 = f32[8,128]{1,0:T(8,128)S(1)} collective-permute-done((f32[8,128]{1,0:T(8,128)S(1)}, f32[8,128]{1,0:T(8,128)S(1)}, u32[]{:S(2)}, u32[]{:S(2)}) %collective-permute-start.7) | collective-permute-done | bytes 4128 | tf_op jit(solution)/shard_map/ppermute | solution.py:286
  25.5 0.6 %multiply_reduce_fusion = f32[]{:T(128)} fusion(f32[8,128]{1,0:T(8,128)S(1)} %collective-permute-done.7, f32[8,128]{1,0:T(8,128)S(1)} %collective-permute-done.6, f32[8,128]{1,0:T(8,128)S(1)} %get-tuple-element.18, f32[8,128]{1,0:T(8,128)S(1)} %collective-permute-done.5), kind=kLoop, calls=%fused_computation | loop fusion | flops 5119 | bytes 16388 | tf_op jit(solution)/shard_map/reduce_max | solution.py:307
  26.1 0.0 collective-permute-done.4
  26.1 0.9 %add.12 = f32[2,256,256]{2,1,0:T(8,128)} add(f32[2,256,256]{2,1,0:T(8,128)S(1)} %get-tuple-element.16, f32[2,256,256]{2,1,0:T(8,128)S(1)} %collective-permute-done.4) | non-fusion elementwise | flops 131072 | bytes 1572864 | tf_op jit(solution)/shard_map/add | solution.py:308
Async XLA Ops:
  0.6 2.6 %collective-permute-start.3 = (bf16[2,128,256]{2,1,0:T(8,128)(2,1)}, bf16[2,128,256]{2,1,0:T(8,128)(2,1)S(1)}, u32[]{:S(2)}, u32[]{:S(2)}) collective-permute-start(bf16[2,128,256]{2,1,0:T(8,128)(2,1)} %spectra.1), channel_id=1, source_target_pairs={{0,1},{1,0},{2,3},{3,2},{4,5},{5,4},{6,7},{7,6},{8,9},{9,8},{10,11... | collective-permute-start | bytes 393224 | tf_op jit(solution)/shard_map/ppermute | solution.py:238
  1.4 1.3 %collective-permute-start = (s32[2]{0:T(128)}, s32[2]{0:T(128)S(1)}, u32[]{:S(2)}, u32[]{:S(2)}) collective-permute-start(s32[2]{0:T(128)} %flags.3), channel_id=1, source_target_pairs={{0,1},{1,0},{2,3},{3,2},{4,5},{5,4},{6,7},{7,6},{8,9},{9,8},{10,11... | collective-permute-start | bytes 32 | tf_op jit(solution)/shard_map/ppermute | solution.py:239
  1.4 1.4 %collective-permute-start.1 = (s32[2]{0:T(128)}, s32[2]{0:T(128)S(1)}, u32[]{:S(2)}, u32[]{:S(2)}) collective-permute-start(s32[2]{0:T(128)} %counts.3), channel_id=1, source_target_pairs={{0,1},{1,0},{2,3},{3,2},{4,5},{5,4},{6,7},{7,6},{8,9},{9,8},{10,11... | collective-permute-start | bytes 32 | tf_op jit(solution)/shard_map/ppermute | solution.py:240
  1.9 1.3 %collective-permute-start.2 = (s32[2]{0:T(128)}, s32[2]{0:T(128)S(1)}, u32[]{:S(2)}, u32[]{:S(2)}) collective-permute-start(s32[2]{0:T(128)} %helper.1), channel_id=1, source_target_pairs={{0,1},{1,0},{2,3},{3,2},{4,5},{5,4},{6,7},{7,6},{8,9},{9,8},{10,11... | collective-permute-start | bytes 32 | tf_op jit(solution)/shard_map/ppermute | solution.py:241
  10.6 15.6 %collective-permute-start.4 = (f32[2,256,256]{2,1,0:T(8,128)S(1)}, f32[2,256,256]{2,1,0:T(8,128)S(1)}, u32[]{:S(2)}, u32[]{:S(2)}) collective-permute-start(f32[2,256,256]{2,1,0:T(8,128)S(1)} %get-tuple-element.17), channel_id=1, source_target_pairs={{0,1},{1,0},{2,3},{3,2},{4,5},{5,4},{6,7},{7,6},{8,9},{9,8},{10,11... | collective-permute-start | bytes 1572872 | tf_op jit(solution)/shard_map/ppermute | solution.py:306
  10.8 11.5 %collective-permute-start.5 = (f32[8,128]{1,0:T(8,128)S(1)}, f32[8,128]{1,0:T(8,128)S(1)}, u32[]{:S(2)}, u32[]{:S(2)}) collective-permute-start(f32[8,128]{1,0:T(8,128)S(1)} %get-tuple-element.19), channel_id=1, source_target_pairs={{4,8},{8,4},{12,16},{16,12},{20,24},{24,20},{28,0},{0,28},{5,9},{9... | collective-permute-start | bytes 12296 | tf_op jit(solution)/shard_map/ppermute | solution.py:284
  11.8 11.4 %collective-permute-start.6 = (f32[8,128]{1,0:T(8,128)S(1)}, f32[8,128]{1,0:T(8,128)S(1)}, u32[]{:S(2)}, u32[]{:S(2)}) collective-permute-start(f32[8,128]{1,0:T(8,128)S(1)} %get-tuple-element.20), channel_id=1, source_target_pairs={{0,4},{4,0},{8,12},{12,8},{16,20},{20,16},{24,28},{28,24},{1,5},{5... | collective-permute-start | bytes 12296 | tf_op jit(solution)/shard_map/ppermute | solution.py:285
  22.2 3.3 %collective-permute-start.7 = (f32[8,128]{1,0:T(8,128)S(1)}, f32[8,128]{1,0:T(8,128)S(1)}, u32[]{:S(2)}, u32[]{:S(2)}) collective-permute-start(f32[8,128]{1,0:T(8,128)S(1)} %get-tuple-element.21), channel_id=1, source_target_pairs={{1,2},{2,1},{3,0},{0,3},{5,6},{6,5},{7,4},{4,7},{9,10},{10,9},{11,... | collective-permute-start | bytes 12296 | tf_op jit(solution)/shard_map/ppermute | solution.py:286
where the time goes:
time: 27.1 us; the launch traced here: 27 us
  starting transfers between devices  13 us (48%)
  Pallas kernels  7.36 us (27%)
  waiting for transfers between devices  4.49 us (17%)
  other arithmetic  1.47 us (5%)
  between operations  0.65 us (2%)
    ppermute x1, starting transfers between devices, on_device(): got.append(lax.ppermute(above, 'blk', pairs(rows, 0)))  10.4 us
    pallas_call x1, Pallas kernels, on_device(): pl.pallas_call(first_kernel, out_shape=[images, jax.ShapeDtypeStruct(kern...  4.55 us
    pallas_call x1, Pallas kernels, on_device(): rest(pflags, pcounts, *far(hotspot_flags, kernel_counts, wrow), kbuf, tbu...  2.81 us
    ppermute x1, waiting for transfers between devices, on_device(): got.append(lax.ppermute(across, 'col', pairs(cols, 1)))  2.28 us
    ppermute x1, starting transfers between devices, on_device(): got = [lax.ppermute(below, 'blk', pairs(rows, 1))]  1.03 us
    ppermute x1, waiting for transfers between devices, on_device(): got.append(lax.ppermute(above, 'blk', pairs(rows, 0)))  0.99 us
    add x1, other arithmetic, on_device(): return (own + other, pending)  0.86 us
    ppermute x1, starting transfers between devices, on_device(): pspectra = lax.ppermute(spectra, 'col', twin)  0.74 us
  transfers between devices with their start and end apart: 8, of which 5 were waited for; matrix products, arithmetic and copies ran while one was open for 2% of the time, Pallas kernels for 0%

commit v1 on v0

v1 whole, which is shorter than its diff:
```python
import functools
import math

import jax
import jax.numpy as jnp
import numpy as np
from jax import lax
from jax.experimental import pallas as pl
from jax.experimental.pallas import tpu as pltpu
from jax.sharding import PartitionSpec as P

Q = 256
KB = 6


def make_table(band_width, length):
    row_index = np.arange(length, dtype=np.int32)[:, None]
    col_index = np.arange(band_width, dtype=np.int32)[None, :] - band_width // 2
    angle = np.mod(row_index * col_index, length).astype(np.float64) * (2.0 * math.pi / length)
    scale = 1.0 / math.sqrt(band_width)
    real = (np.cos(angle) * scale).astype(np.float32).T
    imag = (np.sin(angle) * scale).astype(np.float32).T
    table = np.block([[real, imag], [-imag, real]])
    return jnp.asarray(table).astype(jnp.bfloat16)


def plan(core, flags, counts, kern_total):
    tiles, numbers, firsts, starts = [], [], [], [jnp.int32(0)]
    most = jnp.int32(0)
    for group, (f, c) in enumerate(zip(flags, counts)):
        per = f.shape[0]
        for q in range(per):
            t = lax.rem(core + q, per)
            n = jnp.where(f[t] == 1, kern_total, c[t])
            first = q % 2
            blocks = (n + KB - 1) // KB
            most = jnp.maximum(most, blocks)
            tiles.append(group * per + t)
            numbers.append(n)
            firsts.append(first)
            starts.append(starts[-1] + (blocks - first + 1) // 2)
    return tiles, numbers, firsts, starts, most


def fetch_kernel(flags, counts, helper, weights, spectra, kernels, table, fv, cv, hv, wv, kpart, tbuf, sbuf, sems):
    pairs = [(flags, fv), (counts, cv), (helper, hv), (weights, wv)]
    pairs += [(spectra, sbuf), (kernels.at[pl.ds(0, kpart.shape[0])], kpart), (table, tbuf)]
    copies = [pltpu.make_async_copy(src, dst, sems.at[i]) for i, (src, dst) in enumerate(pairs)]
    for copy in copies:
        copy.start()
    for copy in copies:
        copy.wait()


def split_of(total):
    return total - jnp.maximum((total - 2) // 2, 1)


def run_part(low, high, lists, kbuf, both, ws, img, half, accs, wait):
    a0, a1, b0, b1 = accs[0:2], accs[2:4], accs[4:7], accs[7:10]
    places, numbers, firsts, starts, _ = lists

    def place(i):
        j, start, first, n = places[0], starts[0], firsts[0], numbers[0]
        for q in range(1, len(numbers)):
            take = i >= starts[q]
            j = jnp.where(take, places[q], j)
            start = jnp.where(take, starts[q], start)
            first = jnp.where(take, firsts[q], first)
            n = jnp.where(take, numbers[q], n)
        return j, first + 2 * (i - start), n

    def finish(j, k, n, slot):
        w = jnp.where(k < n, ws[0, k], 0.0)
        fr = pltpu.matmul_pop(b0[slot])
        fi = pltpu.matmul_pop(b1[slot])
        img[j] = img[j] + w * (fr * fr + fi * fi)

    def block(i, carry):
        (j, b, n), (jp, bp, np_), seen = carry
        jn, bn, nn = place(jnp.minimum(i + 1, high - 1))
        seen = wait(bn, seen)
        data = half[...]
        for u in range(KB):
            if u + 2 < KB:
                stage_one(kbuf, both, a0, a1, j, b * KB + u + 2, u % 2)
            else:
                stage_one(kbuf, both, a0, a1, jn, bn * KB + (u + 2 - KB), u % 2)
            pltpu.matmul_acc_lhs(b0[u % 3], data)
            pltpu.matmul_acc_lhs(b1[u % 3], data)
            data = middle(a0, a1, (u + 1) % 2)
            if u < 2:
                finish(jp, bp * KB + KB - 2 + u, np_, (u + 1) % 3)
            else:
                finish(j, b * KB + u - 2, n, (u + 1) % 3)
        half[...] = data
        return (jn, bn, nn), (j, b, n), seen

    here = place(low)
    _, (j, b, n), seen = lax.fori_loop(low, high, block, (here, here, jnp.int32(0)))
    finish(j, b * KB + KB - 2, n, 1)
    finish(j, b * KB + KB - 1, n, 2)
    pltpu.matmul_pop(a0[1])
    pltpu.matmul_pop(a1[1])
    return seen, place


def stage_one(kbuf, both, a0, a1, j, k, slot, first=False):
    width = kbuf.shape[1]
    kb = kbuf[k].astype(jnp.float32)
    kr, ki = kb[:, :width], kb[:, width:]
    sp = both[j].astype(jnp.float32)
    sr, si = sp[:, :width], sp[:, width:]
    band = jnp.concatenate([kr * sr - ki * si, kr * si + ki * sr], 1).astype(jnp.bfloat16)
    load = 0 if first else None
    pltpu.matmul_acc_lhs(a0[slot], band, load_staged_rhs=load)
    pltpu.matmul_acc_lhs(a1[slot], band, load_staged_rhs=load)


def middle(a0, a1, slot):
    hr = pltpu.matmul_pop(a0[slot]).astype(jnp.bfloat16)
    hi = pltpu.matmul_pop(a1[slot]).astype(jnp.bfloat16)
    return jnp.concatenate([hr.T, hi.T], 1)


def push_table(tbuf, length):
    pltpu.matmul_push_rhs(tbuf[:, :length], staging_register=0, mxu_index=0)
    pltpu.matmul_push_rhs(tbuf[:, length:], staging_register=0, mxu_index=1)


def with_accs(body, width, length):
    pl.run_scoped(
        body,
        *[pltpu.ACC(0)((width, length), jnp.float32)] * 2,
        *[pltpu.ACC(1)((width, length), jnp.float32)] * 2,
        *[pltpu.ACC(0)((length, length), jnp.float32)] * 3,
        *[pltpu.ACC(1)((length, length), jnp.float32)] * 3,
    )


def first_kernel(pflags, pcounts, phelper, pspectra, flags, counts, helper, weights, kpart, tbuf, spectra, kernels,
                 img, kbuf, both, base, vertical, across, fl, cn, hm, pfl, pcn, phm, ws, half, ksem, sems):
    tiles, width, _ = spectra.shape
    length = img.shape[1]
    kern_total = kernels.shape[0]
    held = kpart.shape[0] // KB
    core = lax.rem(lax.axis_index("col"), 2)
    pairs = [(flags, fl), (counts, cn), (helper, hm), (pflags, pfl), (pcounts, pcn), (phelper, phm), (weights, ws)]
    copies = [pltpu.make_async_copy(src, dst, sems.at[i]) for i, (src, dst) in enumerate(pairs)]

    def chunk(b):
        part = pl.ds(b * KB, KB)
        return pltpu.make_async_copy(kernels.at[part], kbuf.at[part], ksem.at[b])

    for copy in copies:
        copy.start()
    for b in range(held, kern_total // KB):
        chunk(b).start()

    def body(*accs):
        for acc in accs:
            pltpu.matmul_pop(acc)
        push_table(tbuf, length)
        both[:tiles] = spectra[...]
        both[tiles:] = pspectra[...]
        kbuf[: kpart.shape[0]] = kpart[...]
        a0, a1 = accs[0:2], accs[2:4]
        j0 = lax.rem(core, tiles)
        stage_one(kbuf, both, a0, a1, j0, 0, 0, first=True)
        stage_one(kbuf, both, a0, a1, j0, 1, 1)
        half[...] = middle(a0, a1, 0)
        img[...] = jnp.zeros_like(img)
        for copy in copies:
            copy.wait()
        lists = plan(core, (fl, pfl), (cn, pcn), kern_total)
        total = lists[3][-1]
        split = split_of(total)

        def handed(f, h, direction):
            value = jnp.float32(0)
            for t in range(tiles):
                value = value + jnp.where((f[t] == 1) & (h[t] == direction), jnp.float32(kern_total), 0.0)
            return value

        odd_row = lax.rem(lax.axis_index("blk"), 2)
        direction = jnp.where(core == 0, 1 - odd_row, odd_row)
        mine, twins = handed(fl, hm, direction), handed(pfl, phm, direction)
        line = lax.broadcasted_iota(jnp.int32, vertical.shape, 0)
        vertical[...] = jnp.where(line == core, mine, jnp.where(line == 1 - core, twins, 0.0))
        across[...] = jnp.full(across.shape, handed(fl, hm, 3 - core))
        value = handed(pfl, phm, 3 - core)
        for t in range(tiles):
            value = value + jnp.where(fl[t] == 1, 0, cn[t]).astype(jnp.float32)
        base[...] = jnp.full(base.shape, value)

        def wait(b, seen):
            bit = lax.shift_left(jnp.int32(1), b)
            due = (b >= held) & ((seen & bit) == 0)

            @pl.when(due)
            def _():
                chunk(b).wait()

            return jnp.where(due, seen | bit, seen)

        seen, _ = run_part(jnp.int32(0), split, lists, kbuf, both, ws, img, half, accs, wait)

        def rest(b, seen):
            return wait(b, seen)

        lax.fori_loop(held, kern_total // KB, rest, seen)

    with_accs(body, width, length)


def second_kernel(pflags, pcounts, flags, counts, weights, kbuf, tbuf, both, img_in,
                  own_out, peer_out, fl, cn, pfl, pcn, ws, half, img, sems):
    tiles = own_out.shape[0]
    kern_total, width, _ = kbuf.shape
    length = img.shape[1]
    core = lax.rem(lax.axis_index("col"), 2)
    pairs = [(flags, fl), (counts, cn), (pflags, pfl), (pcounts, pcn), (weights, ws)]
    copies = [pltpu.make_async_copy(src, dst, sems.at[i]) for i, (src, dst) in enumerate(pairs)]
    for copy in copies:
        copy.start()

    def body(*accs):
        push_table(tbuf, length)
        for copy in copies:
            copy.wait()
        lists = plan(core, (fl, pfl), (cn, pcn), kern_total)
        total = lists[3][-1]
        low = split_of(total)
        a0, a1 = accs[0:2], accs[2:4]
        places, numbers, firsts, starts, _ = lists
        j, start, first = places[0], starts[0], firsts[0]
        for q in range(1, len(numbers)):
            take = low >= starts[q]
            j = jnp.where(take, places[q], j)
            start = jnp.where(take, starts[q], start)
            first = jnp.where(take, firsts[q], first)
        k = (first + 2 * (low - start)) * KB
        k = jnp.minimum(k, kern_total - KB)
        stage_one(kbuf, both, a0, a1, j, k, 0, first=True)
        stage_one(kbuf, both, a0, a1, j, k + 1, 1)
        half[...] = middle(a0, a1, 0)
        img[...] = img_in[...]
        run_part(low, total, lists, kbuf, both, ws, img, half, accs, lambda b, seen: seen)
        lane = lax.broadcasted_iota(jnp.int32, (1, kern_total), 1)
        for group, (f, c, dest) in enumerate(((fl, cn, own_out), (pfl, pcn, peer_out))):
            for t in range(tiles):
                n = jnp.where(f[t] == 1, kern_total, c[t])
                weight = jnp.sum(jnp.where(lane < n, weights[...], 0.0), axis=1, keepdims=True)
                dest[t] = img[group * tiles + t].T * (1.0 / weight)

    with_accs(body, width, length)


def final_kernel(scale, own, other, base, across, vertical, twins, image, pending):
    image[...] = own[...] + other[...]
    core = lax.rem(lax.axis_index("col"), 2)
    line = lax.broadcasted_iota(jnp.int32, base.shape, 0)
    both = jnp.where(line == core, vertical[...] + twins[...] + across[...] + base[...], 0.0)
    pending[...] = jnp.sum(both, axis=0, keepdims=True)[:, :1] * scale


def on_device(spectra, kernels, weights, hotspot_flags, helper_map, kernel_counts):
    tiles, width, _ = spectra.shape
    kern_total = kernels.shape[0]
    rows, cols = lax.axis_size("blk"), lax.axis_size("col")
    table = make_table(width, Q)

    def pairs(size, first):
        return [p for i in range(first, size, 2) for p in ((i, (i + 1) % size), ((i + 1) % size, i))]

    twin = pairs(cols, 0)
    pspectra = lax.ppermute(spectra, "col", twin)
    pflags = lax.ppermute(hotspot_flags, "col", twin)
    pcounts = lax.ppermute(kernel_counts, "col", twin)
    phelper = lax.ppermute(helper_map, "col", twin)

    vmem = pl.BlockSpec(memory_space=pltpu.VMEM)
    hbm = pl.BlockSpec(memory_space=pltpu.HBM)

    def far(*arrays):
        return [pltpu.with_memory_space_constraint(x, pltpu.HBM) for x in arrays]

    f32, bf16 = jnp.float32, jnp.bfloat16
    image = jax.ShapeDtypeStruct((tiles, Q, Q), f32)
    wide = jax.ShapeDtypeStruct((8, 128), f32)
    ints = pltpu.SMEM((tiles,), jnp.int32)
    params = pltpu.CompilerParams(vmem_limit_bytes=16 * 2**20)
    ivec = jax.ShapeDtypeStruct((tiles,), jnp.int32)
    fetch = pl.pallas_call(
        fetch_kernel,
        out_shape=[
            ivec,
            ivec,
            ivec,
            jax.ShapeDtypeStruct((1, kern_total), f32),
            jax.ShapeDtypeStruct((3 * KB, width, 2 * width), bf16),
            jax.ShapeDtypeStruct(table.shape, bf16),
            jax.ShapeDtypeStruct(spectra.shape, bf16),
        ],
        in_specs=[hbm] * 7,
        out_specs=[vmem] * 7,
        scratch_shapes=[pltpu.SemaphoreType.DMA((7,))],
        compiler_params=params,
        cost_estimate=pl.CostEstimate(flops=10**9, transcendentals=0, bytes_accessed=10**6),
        name="fetch",
    )
    fv, cv, hv, wv, kpart, tbuf, sbuf = fetch(
        *far(hotspot_flags, kernel_counts, helper_map, weights.reshape(1, -1), spectra, kernels, table)
    )
    row_smem = pltpu.SMEM((1, kern_total), f32)
    half = pltpu.VMEM((Q, 2 * width), bf16)
    images = jax.ShapeDtypeStruct((2 * tiles, Q, Q), f32)
    cost = pl.CostEstimate(flops=10**10, transcendentals=0, bytes_accessed=10**6)
    work = pl.pallas_call(
        first_kernel,
        out_shape=[
            images,
            jax.ShapeDtypeStruct(kernels.shape, bf16),
            jax.ShapeDtypeStruct((2 * tiles, width, 2 * width), bf16),
            wide,
            wide,
            wide,
        ],
        in_specs=[vmem] * 11 + [hbm],
        out_specs=[vmem] * 6,
        scratch_shapes=[
            *[ints] * 6,
            row_smem,
            half,
            pltpu.SemaphoreType.DMA((kern_total // KB,)),
            pltpu.SemaphoreType.DMA((7,)),
        ],
        compiler_params=params,
        cost_estimate=cost,
        name="work",
    )
    img, kbuf, both, base, vertical, across = work(
        pflags, pcounts, phelper, pspectra, fv, cv, hv, wv, kpart, tbuf, sbuf, *far(kernels)
    )
    rounds = []
    for parity in range(2):
        for i, j in pairs(rows, 1 - parity):
            rounds += [(i * cols + c, j * cols + c) for c in range(parity, cols, 2)]
    vertical = lax.ppermute(vertical, ("blk", "col"), rounds)
    across = lax.ppermute(across, "col", pairs(cols, 1))
    rest = pl.pallas_call(
        second_kernel,
        out_shape=[image, image],
        in_specs=[vmem] * 9,
        out_specs=[vmem] * 2,
        scratch_shapes=[
            *[ints] * 4,
            row_smem,
            half,
            pltpu.VMEM((2 * tiles, Q, Q), f32),
            pltpu.SemaphoreType.DMA((5,)),
        ],
        compiler_params=params,
        cost_estimate=cost,
        name="rest",
    )
    own, peer = rest(pflags, pcounts, fv, cv, wv, kbuf, tbuf, both, img)
    other = lax.ppermute(peer, "col", twin)
    twins = lax.ppermute(vertical, "col", twin)
    return tuple(
        pl.pallas_call(
            functools.partial(final_kernel, 1.0 / kern_total),
            out_shape=[image, jax.ShapeDtypeStruct((1, 1), f32)],
            in_specs=[vmem] * 6,
            out_specs=[vmem] * 2,
            compiler_params=params,
            name="final",
        )(own, other, base, across, vertical, twins)
    )


def solution(mesh):
    in_specs = (
        P(("blk", "col"), None, None),
        P(),
        P(),
        P(("blk", "col")),
        P(("blk", "col")),
        P(("blk", "col")),
    )
    out_specs = (P(("blk", "col"), None, None), P("blk", "col"))
    return jax.shard_map(on_device, mesh=mesh, in_specs=in_specs, out_specs=out_specs, check_vma=False)
```

time: 27.1 us -> 24.3 us (0.90)
  the two profiles are of different devices: /device:TPU:19 before, /device:TPU:27 now
where the time goes in v1:
time: 24.3 us; the launch traced here: 24.2 us
  Pallas kernels  15.6 us (64%)
  starting transfers between devices  4.35 us (18%)
  waiting for transfers between devices  3.58 us (15%)
  between operations  0.69 us (3%)
    pallas_call x1, Pallas kernels, on_device(): work(pflags, pcounts, phelper, pspectra, fv, cv, hv, wv, kpart, tbuf, sbu...  7.69 us
    pallas_call x1, Pallas kernels, on_device(): own, peer = rest(pflags, pcounts, fv, cv, wv, kbuf, tbuf, both, img)  5.52 us
    ppermute x1, waiting for transfers between devices, on_device(): vertical = lax.ppermute(vertical, ('blk', 'col'), rounds)  2.75 us
    ppermute x1, starting transfers between devices, on_device(): twins = lax.ppermute(vertical, 'col', twin)  1.83 us
    pallas_call x1, Pallas kernels, on_device(): fetch(*far(hotspot_flags, kernel_counts, helper_map, weights.reshape(1, -...  1.49 us
    ppermute x1, starting transfers between devices, on_device(): other = lax.ppermute(peer, 'col', twin)  1.19 us
    pallas_call x1, Pallas kernels, on_device(): pl.pallas_call(functools.partial(final_kernel, 1.0 / kern_total), out_sha...  0.85 us
    ppermute x1, waiting for transfers between devices, on_device(): twins = lax.ppermute(vertical, 'col', twin)  0.82 us
  transfers between devices with their start and end apart: 8, of which 2 were waited for; matrix products, arithmetic and copies ran while one was open for 0% of the time, Pallas kernels for 6%

profile of v1, /device:TPU:27, one launch (start us, length us, event | category | flops | bytes accessed | tf_op | source)
XLA Modules:
  0.0 24.2 jit_solution(18283849300454805952)
XLA Ops:
  0.6 0.7 %collective-permute-start.3 = (bf16[2,128,256]{2,1,0:T(8,128)(2,1)}, bf16[2,128,256]{2,1,0:T(8,128)(2,1)S(1)}, u32[]{:S(2)}, u32[]{:S(2)}) collective-permute-start(bf16[2,128,256]{2,1,0:T(8,128)(2,1)} %spectra.1), channel_id=1, source_target_pairs={{0,1},{1,0},{2,3},{3,2},{4,5},{5,4},{6,7},{7,6},{8,9},{9,8},{10,11... | collective-permute-start | bytes 393224 | tf_op jit(solution)/shard_map/ppermute | solution.py:277
  1.4 0.1 collective-permute-start
  1.4 0.4 %collective-permute-start.2 = (s32[2]{0:T(128)}, s32[2]{0:T(128)S(1)}, u32[]{:S(2)}, u32[]{:S(2)}) collective-permute-start(s32[2]{0:T(128)} %helper.1), channel_id=1, source_target_pairs={{0,1},{1,0},{2,3},{3,2},{4,5},{5,4},{6,7},{7,6},{8,9},{9,8},{10,11... | collective-permute-start | bytes 32 | tf_op jit(solution)/shard_map/ppermute | solution.py:280
  1.9 0.1 collective-permute-start.1
  2.0 1.5 %fetch.1 = (s32[2]{0:T(128)S(1)}, s32[2]{0:T(128)S(1)}, s32[2]{0:T(128)S(1)}, f32[1,60]{1,0:T(1,128)S(1)}, bf16[18,128,256]{2,1,0:T(8,128)(2,1)S(1)}, /*index=5*...) custom-call(s32[2]{0:T(128)} %flags.1, s32[2]{0:T(128)} %counts.1, s32[2]{0:T(128)} %helper.1, f32[1,60]{1,0:T(1,128)} %bitcast.1, ...), custom_call_target="tpu_custom_call" | custom-call | flops 1000000000 | bytes 1000000 | tf_op jit(solution)/shard_map/fetch/pallas_call | solution.py:312
  3.5 0.0 collective-permute-done.pflags
  3.5 0.0 collective-permute-done.2.phelper
  3.5 0.0 collective-permute-done.1.pcounts
  3.5 0.0 collective-permute-done.3.pspectra
  3.5 7.7 %work.1 = (f32[4,256,256]{2,1,0:T(8,128)S(1)}, bf16[60,128,256]{2,1,0:T(8,128)(2,1)S(1)}, bf16[4,128,256]{2,1,0:T(8,128)(2,1)S(1)}, f32[8,128]{1,0:T(8,128)S(1)}...) custom-call(s32[2]{0:T(128)S(1)} %collective-permute-done.pflags, s32[2]{0:T(128)S(1)} %collective-permute-done.1.pcounts, ...), custom_call_target="tpu_custom_call" | custom-call | flops 10000000000 | bytes 1000000 | tf_op jit(solution)/shard_map/work/pallas_call | solution.py:342
  11.2 5.5 %rest.1 = (f32[2,256,256]{2,1,0:T(8,128)S(1)}, f32[2,256,256]{2,1,0:T(8,128)S(1)}) custom-call(s32[2]{0:T(128)S(1)} %collective-permute-done.pflags, s32[2]{0:T(128)S(1)} %collective-permute-done.1.pcounts, s32[2]{0:T(128)S(1)} %get-tuple-element.17.flags, s32[2]{0:T(128)S(1)} %get-tuple-element.18.counts, f32[1,60]{1,0:T(1,128)S(1)} %get-tuple-element.19.weights, ...), custom_call_target="tpu_custom_call" | custom-call | flops 10000000000 | bytes 1000000 | tf_op jit(solution)/shard_map/rest/pallas_call | solution.py:367
  16.7 1.2 %collective-permute-start.4 = (f32[2,256,256]{2,1,0:T(8,128)S(1)}, f32[2,256,256]{2,1,0:T(8,128)S(1)}, u32[]{:S(2)}, u32[]{:S(2)}) collective-permute-start(f32[2,256,256]{2,1,0:T(8,128)S(1)} %get-tuple-element.28), channel_id=1, source_target_pairs={{0,1},{1,0},{2,3},{3,2},{4,5},{5,4},{6,7},{7,6},{8,9},{9,8},{10,11... | collective-permute-start | bytes 1572872 | tf_op jit(solution)/shard_map/ppermute | solution.py:368
  17.9 0.0 collective-permute-start.6
  17.9 0.0 collective-permute-start.5
  17.9 2.7 %collective-permute-done.6.vertical = f32[8,128]{1,0:T(8,128)S(1)} collective-permute-done((f32[8,128]{1,0:T(8,128)S(1)}, f32[8,128]{1,0:T(8,128)S(1)}, u32[]{:S(2)}, u32[]{:S(2)}) %collective-permute-start.6) | collective-permute-done | bytes 4128 | tf_op jit(solution)/shard_map/ppermute | solution.py:349
  20.7 1.8 %collective-permute-start.7 = (f32[8,128]{1,0:T(8,128)S(1)}, f32[8,128]{1,0:T(8,128)S(1)}, u32[]{:S(2)}, u32[]{:S(2)}) collective-permute-start(f32[8,128]{1,0:T(8,128)S(1)} %collective-permute-done.6.vertical), channel_id=1, source_target_pairs={{0,1},{1,0},{2,3},{3,2},{4,5},{5,4},{6,7},{7,6},{8,9},{9,8},{10,11... | collective-permute-start | bytes 12296 | tf_op jit(solution)/shard_map/ppermute | solution.py:369
  22.5 0.0 collective-permute-done.5.across
  22.5 0.8 %collective-permute-done.7.twins = f32[8,128]{1,0:T(8,128)S(1)} collective-permute-done((f32[8,128]{1,0:T(8,128)S(1)}, f32[8,128]{1,0:T(8,128)S(1)}, u32[]{:S(2)}, u32[]{:S(2)}) %collective-permute-start.7) | collective-permute-done | bytes 4128 | tf_op jit(solution)/shard_map/ppermute | solution.py:369
  23.3 0.0 collective-permute-done.4.other
  23.3 0.8 %final.1 = (f32[2,256,256]{2,1,0:T(8,128)}, f32[1,1]{1,0:T(1,128)}) custom-call(f32[2,256,256]{2,1,0:T(8,128)S(1)} %get-tuple-element.27.own, f32[2,256,256]{2,1,0:T(8,128)S(1)} %collective-permute-done.4.other, f32[8,128]{1,0:T(8,128)S(1)} %get-tuple-element.29.base, f32[8,128]{1,0:T(8,128)S(1)} %collective-permute-done.5.across, ...), custom_call_target="tpu_custom_call" | custom-call | tf_op jit(solution)/shard_map/final/pallas_call | solution.py:371
Async XLA Ops:
  0.6 2.9 %collective-permute-start.3 = (bf16[2,128,256]{2,1,0:T(8,128)(2,1)}, bf16[2,128,256]{2,1,0:T(8,128)(2,1)S(1)}, u32[]{:S(2)}, u32[]{:S(2)}) collective-permute-start(bf16[2,128,256]{2,1,0:T(8,128)(2,1)} %spectra.1), channel_id=1, source_target_pairs={{0,1},{1,0},{2,3},{3,2},{4,5},{5,4},{6,7},{7,6},{8,9},{9,8},{10,11... | collective-permute-start | bytes 393224 | tf_op jit(solution)/shard_map/ppermute | solution.py:277
  1.4 2.1 %collective-permute-start = (s32[2]{0:T(128)}, s32[2]{0:T(128)S(1)}, u32[]{:S(2)}, u32[]{:S(2)}) collective-permute-start(s32[2]{0:T(128)} %flags.1), channel_id=1, source_target_pairs={{0,1},{1,0},{2,3},{3,2},{4,5},{5,4},{6,7},{7,6},{8,9},{9,8},{10,11... | collective-permute-start | bytes 32 | tf_op jit(solution)/shard_map/ppermute | solution.py:278
  1.4 2.0 %collective-permute-start.2 = (s32[2]{0:T(128)}, s32[2]{0:T(128)S(1)}, u32[]{:S(2)}, u32[]{:S(2)}) collective-permute-start(s32[2]{0:T(128)} %helper.1), channel_id=1, source_target_pairs={{0,1},{1,0},{2,3},{3,2},{4,5},{5,4},{6,7},{7,6},{8,9},{9,8},{10,11... | collective-permute-start | bytes 32 | tf_op jit(solution)/shard_map/ppermute | solution.py:280
  1.9 1.6 %collective-permute-start.1 = (s32[2]{0:T(128)}, s32[2]{0:T(128)S(1)}, u32[]{:S(2)}, u32[]{:S(2)}) collective-permute-start(s32[2]{0:T(128)} %counts.1), channel_id=1, source_target_pairs={{0,1},{1,0},{2,3},{3,2},{4,5},{5,4},{6,7},{7,6},{8,9},{9,8},{10,11... | collective-permute-start | bytes 32 | tf_op jit(solution)/shard_map/ppermute | solution.py:279
  16.7 6.6 %collective-permute-start.4 = (f32[2,256,256]{2,1,0:T(8,128)S(1)}, f32[2,256,256]{2,1,0:T(8,128)S(1)}, u32[]{:S(2)}, u32[]{:S(2)}) collective-permute-start(f32[2,256,256]{2,1,0:T(8,128)S(1)} %get-tuple-element.28), channel_id=1, source_target_pairs={{0,1},{1,0},{2,3},{3,2},{4,5},{5,4},{6,7},{7,6},{8,9},{9,8},{10,11... | collective-permute-start | bytes 1572872 | tf_op jit(solution)/shard_map/ppermute | solution.py:368
  17.9 2.8 %collective-permute-start.6 = (f32[8,128]{1,0:T(8,128)S(1)}, f32[8,128]{1,0:T(8,128)S(1)}, u32[]{:S(2)}, u32[]{:S(2)}) collective-permute-start(f32[8,128]{1,0:T(8,128)S(1)} %get-tuple-element.31), channel_id=1, source_target_pairs={{4,8},{6,10},{8,4},{10,6},{12,16},{14,18},{16,12},{18,14},{20,24},... | collective-permute-start | bytes 12296 | tf_op jit(solution)/shard_map/ppermute | solution.py:349
  17.9 4.6 %collective-permute-start.5 = (f32[8,128]{1,0:T(8,128)S(1)}, f32[8,128]{1,0:T(8,128)S(1)}, u32[]{:S(2)}, u32[]{:S(2)}) collective-permute-start(f32[8,128]{1,0:T(8,128)S(1)} %get-tuple-element.30), channel_id=1, source_target_pairs={{1,2},{2,1},{3,0},{0,3},{5,6},{6,5},{7,4},{4,7},{9,10},{10,9},{11,... | collective-permute-start | bytes 12296 | tf_op jit(solution)/shard_map/ppermute | solution.py:350
  20.7 2.7 %collective-permute-start.7 = (f32[8,128]{1,0:T(8,128)S(1)}, f32[8,128]{1,0:T(8,128)S(1)}, u32[]{:S(2)}, u32[]{:S(2)}) collective-permute-start(f32[8,128]{1,0:T(8,128)S(1)} %collective-permute-done.6.vertical), channel_id=1, source_target_pairs={{0,1},{1,0},{2,3},{3,2},{4,5},{5,4},{6,7},{7,6},{8,9},{9,8},{10,11... | collective-permute-start | bytes 12296 | tf_op jit(solution)/shard_map/ppermute | solution.py:369

commit v2 on v1

--- a/solution.py
+++ b/solution.py
@@ -251,13 +251,13 @@
             for t in range(tiles):
                 n = jnp.where(f[t] == 1, kern_total, c[t])
                 weight = jnp.sum(jnp.where(lane < n, weights[...], 0.0), axis=1, keepdims=True)
-                dest[t] = img[group * tiles + t].T * (1.0 / weight)
+                dest[t] = (img[group * tiles + t].T * (1.0 / weight)).astype(dest.dtype)
 
     with_accs(body, width, length)
 
 
 def final_kernel(scale, own, other, base, across, vertical, twins, image, pending):
-    image[...] = own[...] + other[...]
+    image[...] = own[...] + other[...].astype(own.dtype)
     core = lax.rem(lax.axis_index("col"), 2)
     line = lax.broadcasted_iota(jnp.int32, base.shape, 0)
     both = jnp.where(line == core, vertical[...] + twins[...] + across[...] + base[...], 0.0)
@@ -298,7 +298,7 @@
             ivec,
             ivec,
             jax.ShapeDtypeStruct((1, kern_total), f32),
-            jax.ShapeDtypeStruct((3 * KB, width, 2 * width), bf16),
+            jax.ShapeDtypeStruct((2 * KB, width, 2 * width), bf16),
             jax.ShapeDtypeStruct(table.shape, bf16),
             jax.ShapeDtypeStruct(spectra.shape, bf16),
         ],
@@ -350,7 +350,7 @@
     across = lax.ppermute(across, "col", pairs(cols, 1))
     rest = pl.pallas_call(
         second_kernel,
-        out_shape=[image, image],
+        out_shape=[image, jax.ShapeDtypeStruct(image.shape, bf16)],
         in_specs=[vmem] * 9,
         out_specs=[vmem] * 2,
         scratch_shapes=[

time: 24.3 us -> 24.3 us (level)
  no operation moved by 1% of the time
where the time goes in v2:
time: 24.3 us; the launch traced here: 24.1 us
  Pallas kernels  15.5 us (64%)
  starting transfers between devices  4.35 us (18%)
  waiting for transfers between devices  3.58 us (15%)
  between operations  0.69 us (3%)
    pallas_call x1, Pallas kernels, on_device(): work(pflags, pcounts, phelper, pspectra, fv, cv, hv, wv, kpart, tbuf, sbu...  7.76 us
    pallas_call x1, Pallas kernels, on_device(): own, peer = rest(pflags, pcounts, fv, cv, wv, kbuf, tbuf, both, img)  5.52 us
    ppermute x1, waiting for transfers between devices, on_device(): vertical = lax.ppermute(vertical, ('blk', 'col'), rounds)  2.75 us
    ppermute x1, starting transfers between devices, on_device(): twins = lax.ppermute(vertical, 'col', twin)  1.83 us
    pallas_call x1, Pallas kernels, on_device(): fetch(*far(hotspot_flags, kernel_counts, helper_map, weights.reshape(1, -...  1.37 us
    ppermute x1, starting transfers between devices, on_device(): other = lax.ppermute(peer, 'col', twin)  1.19 us
    pallas_call x1, Pallas kernels, on_device(): pl.pallas_call(functools.partial(final_kernel, 1.0 / kern_total), out_sha...  0.84 us
    ppermute x1, waiting for transfers between devices, on_device(): twins = lax.ppermute(vertical, 'col', twin)  0.82 us
  transfers between devices with their start and end apart: 8, of which 2 were waited for; matrix products, arithmetic and copies ran while one was open for 0% of the time, Pallas kernels for 6%

profile of v2, /device:TPU:27, one launch (start us, length us, event | category | flops | bytes accessed | tf_op | source)
XLA Modules:
  0.0 24.1 jit_solution(6592932404454358302)
XLA Ops:
  0.6 0.7 %collective-permute-start.3 = (bf16[2,128,256]{2,1,0:T(8,128)(2,1)}, bf16[2,128,256]{2,1,0:T(8,128)(2,1)S(1)}, u32[]{:S(2)}, u32[]{:S(2)}) collective-permute-start(bf16[2,128,256]{2,1,0:T(8,128)(2,1)} %spectra.1), channel_id=1, source_target_pairs={{0,1},{1,0},{2,3},{3,2},{4,5},{5,4},{6,7},{7,6},{8,9},{9,8},{10,11... | collective-permute-start | bytes 393224 | tf_op jit(solution)/shard_map/ppermute | solution.py:277
  1.4 0.1 collective-permute-start
  1.4 0.4 %collective-permute-start.2 = (s32[2]{0:T(128)}, s32[2]{0:T(128)S(1)}, u32[]{:S(2)}, u32[]{:S(2)}) collective-permute-start(s32[2]{0:T(128)} %helper.1), channel_id=1, source_target_pairs={{0,1},{1,0},{2,3},{3,2},{4,5},{5,4},{6,7},{7,6},{8,9},{9,8},{10,11... | collective-permute-start | bytes 32 | tf_op jit(solution)/shard_map/ppermute | solution.py:280
  1.9 0.1 collective-permute-start.1
  2.0 1.4 %fetch.1 = (s32[2]{0:T(128)S(1)}, s32[2]{0:T(128)S(1)}, s32[2]{0:T(128)S(1)}, f32[1,60]{1,0:T(1,128)S(1)}, bf16[12,128,256]{2,1,0:T(8,128)(2,1)S(1)}, /*index=5*...) custom-call(s32[2]{0:T(128)} %flags.1, s32[2]{0:T(128)} %counts.1, s32[2]{0:T(128)} %helper.1, f32[1,60]{1,0:T(1,128)} %bitcast.1, ...), custom_call_target="tpu_custom_call" | custom-call | flops 1000000000 | bytes 1000000 | tf_op jit(solution)/shard_map/fetch/pallas_call | solution.py:312
  3.3 0.0 collective-permute-done.pflags
  3.4 0.0 collective-permute-done.2.phelper
  3.4 0.0 collective-permute-done.1.pcounts
  3.4 0.0 collective-permute-done.3.pspectra
  3.4 7.8 %work.1 = (f32[4,256,256]{2,1,0:T(8,128)S(1)}, bf16[60,128,256]{2,1,0:T(8,128)(2,1)S(1)}, bf16[4,128,256]{2,1,0:T(8,128)(2,1)S(1)}, f32[8,128]{1,0:T(8,128)S(1)}...) custom-call(s32[2]{0:T(128)S(1)} %collective-permute-done.pflags, s32[2]{0:T(128)S(1)} %collective-permute-done.1.pcounts, ...), custom_call_target="tpu_custom_call" | custom-call | flops 10000000000 | bytes 1000000 | tf_op jit(solution)/shard_map/work/pallas_call | solution.py:342
  11.2 5.5 %rest.1 = (f32[2,256,256]{2,1,0:T(8,128)S(1)}, bf16[2,256,256]{2,1,0:T(8,128)(2,1)S(1)}) custom-call(s32[2]{0:T(128)S(1)} %collective-permute-done.pflags, s32[2]{0:T(128)S(1)} %collective-permute-done.1.pcounts, s32[2]{0:T(128)S(1)} %get-tuple-element.17.flags, s32[2]{0:T(128)S(1)} %get-tuple-element.18.counts, f32[1,60]{1,0:T(1,128)S(1)} %get-tuple-element.19.weights, ...), custom_call_target="tpu_custom_call" | custom-call | flops 10000000000 | bytes 1000000 | tf_op jit(solution)/shard_map/rest/pallas_call | solution.py:367
  16.7 1.2 %collective-permute-start.4 = (bf16[2,256,256]{2,1,0:T(8,128)(2,1)S(1)}, bf16[2,256,256]{2,1,0:T(8,128)(2,1)S(1)}, u32[]{:S(2)}, u32[]{:S(2)}) collective-permute-start(bf16[2,256,256]{2,1,0:T(8,128)(2,1)S(1)} %get-tuple-element.28), channel_id=1, source_target_pairs={{0,1},{1,0},{2,3},{3,2},{4,5},{5,4},{6,7},{7,6},{8,9},{9,8},{10,11... | collective-permute-start | bytes 786440 | tf_op jit(solution)/shard_map/ppermute | solution.py:368
  17.9 0.0 collective-permute-start.6
  17.9 0.0 collective-permute-start.5
  17.9 2.7 %collective-permute-done.6.vertical = f32[8,128]{1,0:T(8,128)S(1)} collective-permute-done((f32[8,128]{1,0:T(8,128)S(1)}, f32[8,128]{1,0:T(8,128)S(1)}, u32[]{:S(2)}, u32[]{:S(2)}) %collective-permute-start.6) | collective-permute-done | bytes 4128 | tf_op jit(solution)/shard_map/ppermute | solution.py:349
  20.6 1.8 %collective-permute-start.7 = (f32[8,128]{1,0:T(8,128)S(1)}, f32[8,128]{1,0:T(8,128)S(1)}, u32[]{:S(2)}, u32[]{:S(2)}) collective-permute-start(f32[8,128]{1,0:T(8,128)S(1)} %collective-permute-done.6.vertical), channel_id=1, source_target_pairs={{0,1},{1,0},{2,3},{3,2},{4,5},{5,4},{6,7},{7,6},{8,9},{9,8},{10,11... | collective-permute-start | bytes 12296 | tf_op jit(solution)/shard_map/ppermute | solution.py:369
  22.5 0.0 collective-permute-done.5.across
  22.5 0.8 %collective-permute-done.7.twins = f32[8,128]{1,0:T(8,128)S(1)} collective-permute-done((f32[8,128]{1,0:T(8,128)S(1)}, f32[8,128]{1,0:T(8,128)S(1)}, u32[]{:S(2)}, u32[]{:S(2)}) %collective-permute-start.7) | collective-permute-done | bytes 4128 | tf_op jit(solution)/shard_map/ppermute | solution.py:369
  23.3 0.0 collective-permute-done.4.other
  23.3 0.8 %final.1 = (f32[2,256,256]{2,1,0:T(8,128)}, f32[1,1]{1,0:T(1,128)}) custom-call(f32[2,256,256]{2,1,0:T(8,128)S(1)} %get-tuple-element.27.own, bf16[2,256,256]{2,1,0:T(8,128)(2,1)S(1)} %collective-permute-done.4.other, f32[8,128]{1,0:T(8,128)S(1)} %get-tuple-element.29.base, f32[8,128]{1,0:T(8,128)S(1)} %collective-permute-done.5.across, ...), custom_call_target="tpu_custom_call" | custom-call | tf_op jit(solution)/shard_map/final/pallas_call | solution.py:371
Async XLA Ops:
  0.6 2.7 %collective-permute-start.3 = (bf16[2,128,256]{2,1,0:T(8,128)(2,1)}, bf16[2,128,256]{2,1,0:T(8,128)(2,1)S(1)}, u32[]{:S(2)}, u32[]{:S(2)}) collective-permute-start(bf16[2,128,256]{2,1,0:T(8,128)(2,1)} %spectra.1), channel_id=1, source_target_pairs={{0,1},{1,0},{2,3},{3,2},{4,5},{5,4},{6,7},{7,6},{8,9},{9,8},{10,11... | collective-permute-start | bytes 393224 | tf_op jit(solution)/shard_map/ppermute | solution.py:277
  1.4 2.0 %collective-permute-start = (s32[2]{0:T(128)}, s32[2]{0:T(128)S(1)}, u32[]{:S(2)}, u32[]{:S(2)}) collective-permute-start(s32[2]{0:T(128)} %flags.1), channel_id=1, source_target_pairs={{0,1},{1,0},{2,3},{3,2},{4,5},{5,4},{6,7},{7,6},{8,9},{9,8},{10,11... | collective-permute-start | bytes 32 | tf_op jit(solution)/shard_map/ppermute | solution.py:278
  1.4 1.9 %collective-permute-start.2 = (s32[2]{0:T(128)}, s32[2]{0:T(128)S(1)}, u32[]{:S(2)}, u32[]{:S(2)}) collective-permute-start(s32[2]{0:T(128)} %helper.1), channel_id=1, source_target_pairs={{0,1},{1,0},{2,3},{3,2},{4,5},{5,4},{6,7},{7,6},{8,9},{9,8},{10,11... | collective-permute-start | bytes 32 | tf_op jit(solution)/shard_map/ppermute | solution.py:280
  1.9 1.5 %collective-permute-start.1 = (s32[2]{0:T(128)}, s32[2]{0:T(128)S(1)}, u32[]{:S(2)}, u32[]{:S(2)}) collective-permute-start(s32[2]{0:T(128)} %counts.1), channel_id=1, source_target_pairs={{0,1},{1,0},{2,3},{3,2},{4,5},{5,4},{6,7},{7,6},{8,9},{9,8},{10,11... | collective-permute-start | bytes 32 | tf_op jit(solution)/shard_map/ppermute | solution.py:279
  16.7 6.6 %collective-permute-start.4 = (bf16[2,256,256]{2,1,0:T(8,128)(2,1)S(1)}, bf16[2,256,256]{2,1,0:T(8,128)(2,1)S(1)}, u32[]{:S(2)}, u32[]{:S(2)}) collective-permute-start(bf16[2,256,256]{2,1,0:T(8,128)(2,1)S(1)} %get-tuple-element.28), channel_id=1, source_target_pairs={{0,1},{1,0},{2,3},{3,2},{4,5},{5,4},{6,7},{7,6},{8,9},{9,8},{10,11... | collective-permute-start | bytes 786440 | tf_op jit(solution)/shard_map/ppermute | solution.py:368
  17.9 2.8 %collective-permute-start.6 = (f32[8,128]{1,0:T(8,128)S(1)}, f32[8,128]{1,0:T(8,128)S(1)}, u32[]{:S(2)}, u32[]{:S(2)}) collective-permute-start(f32[8,128]{1,0:T(8,128)S(1)} %get-tuple-element.31), channel_id=1, source_target_pairs={{4,8},{6,10},{8,4},{10,6},{12,16},{14,18},{16,12},{18,14},{20,24},... | collective-permute-start | bytes 12296 | tf_op jit(solution)/shard_map/ppermute | solution.py:349
  17.9 4.6 %collective-permute-start.5 = (f32[8,128]{1,0:T(8,128)S(1)}, f32[8,128]{1,0:T(8,128)S(1)}, u32[]{:S(2)}, u32[]{:S(2)}) collective-permute-start(f32[8,128]{1,0:T(8,128)S(1)} %get-tuple-element.30), channel_id=1, source_target_pairs={{1,2},{2,1},{3,0},{0,3},{5,6},{6,5},{7,4},{4,7},{9,10},{10,9},{11,... | collective-permute-start | bytes 12296 | tf_op jit(solution)/shard_map/ppermute | solution.py:350
  20.6 2.7 %collective-permute-start.7 = (f32[8,128]{1,0:T(8,128)S(1)}, f32[8,128]{1,0:T(8,128)S(1)}, u32[]{:S(2)}, u32[]{:S(2)}) collective-permute-start(f32[8,128]{1,0:T(8,128)S(1)} %collective-permute-done.6.vertical), channel_id=1, source_target_pairs={{0,1},{1,0},{2,3},{3,2},{4,5},{5,4},{6,7},{7,6},{8,9},{9,8},{10,11... | collective-permute-start | bytes 12296 | tf_op jit(solution)/shard_map/ppermute | solution.py:369
